TPU v7x, 32 devices: a whole 2x2x4 slice. The times are simulated.
32 devices in a mesh: gx: 4 (over z), gy: 4 (over x, core), gz: 2 (over y).
Axes of the slice: x: 2, y: 2, z: 4, core: 2. Of those that a mesh axis runs over, the one named last changes fastest.
Arguments:
- right_side: bfloat16 [16, 256, 512], P('gz', 'gx', 'gy'), may hold values from -6 to 6
- phase_mask: int32 [16, 256, 512], P('gz', 'gx', 'gy'), may hold values from 0 to 1, as said below
Outputs:
- pressure: float32 [16, 256, 512], P('gz', 'gx', 'gy')
- scaled_residual: float32 [16, 256, 512], P('gz', 'gx', 'gy')
Inputs may be any that keep to these rules, and one draw needn't show every extreme that they name: `phase_mask`: 0 for a gas cell, 1 for a liquid cell.
All inputs are finite; a program needn't handle non-finite values.
Results may differ from a plain program's by a relative error of at most 0.0004.
Values may be sent and summed in bfloat16 or wider, within the bound.
A program may use at most 64 MiB of HBM per device.

v0:
```python
import jax
import jax.numpy as jnp
from jax import lax
from jax.sharding import PartitionSpec as P

ITERS = 3
density_ratio = 1000.0
mass_shift = 0.05


def padded_2(cells, sides, width):
    for axis, dim in sides:
        count = lax.axis_size(axis)
        head = lax.slice_in_dim(cells, 0, width, axis=dim)
        tail = lax.slice_in_dim(cells, cells.shape[dim] - width, cells.shape[dim], axis=dim)
        cells = jnp.concatenate(
            [
                lax.ppermute(tail, axis, [(i, (i + 1) % count) for i in range(count)]),
                cells,
                lax.ppermute(head, axis, [((i + 1) % count, i) for i in range(count)]),
            ],
            axis=dim,
        )
    return cells


def neighbour(padded, axis, start):
    window = [slice(1, -1), slice(1, -1), slice(1, -1)]
    length = padded.shape[axis] - 2
    window[axis] = slice(start, start + length)
    return padded[tuple(window)]


def centre(padded):
    return padded[1:-1, 1:-1, 1:-1]


def apply_padded(field, padded, weights):
    total = mass_shift * field
    for weight, axis, start in weights:
        total = total + weight * (field - neighbour(padded, axis, start))
    return total


def operate(field, weights):
    padded = padded_2(field, (("gx", 1), ("gy", 2), ("gz", 0)), 1)
    return apply_padded(field, padded, weights)


def products(first, second, third, fourth):
    return lax.psum((jnp.sum(first * second), jnp.sum(third * fourth)), ("gx", "gy", "gz"))


def build_weights(density_padded):
    density = centre(density_padded)
    weights = []
    diagonal = jnp.full(density.shape, mass_shift, jnp.float32)
    for axis in range(3):
        for start in (0, 2):
            weight = 2.0 / (density + neighbour(density_padded, axis, start))
            weights.append((weight, axis, start))
            diagonal = diagonal + weight
    return (weights, diagonal)


def on_device(right_side, phase_mask):
    mask_padded = padded_2(phase_mask, (("gx", 1), ("gy", 2), ("gz", 0)), 1)
    density_padded = 1.0 + (density_ratio - 1.0) * mask_padded.astype(jnp.float32)
    weights, diagonal = build_weights(density_padded)
    source = diagonal * right_side.astype(jnp.float32)
    smoothed = source / diagonal
    first_padded = padded_2(
        smoothed.astype(jnp.bfloat16), (("gx", 1), ("gy", 2), ("gz", 0)), 1
    ).astype(smoothed.dtype)
    applied = apply_padded(smoothed, first_padded, weights)
    pressure = jnp.zeros_like(source)
    residual = source
    direction = smoothed
    direction_image = applied
    scaled_update = smoothed
    twice_update = applied
    energy_old = jnp.float32(1.0)
    step_old = jnp.float32(1.0)
    for iteration in range(ITERS):
        energy, curvature = products(residual, smoothed, applied, smoothed)
        final_turn = iteration + 1 == ITERS
        if not final_turn:
            scaled_applied = applied / diagonal
            applied_twice = operate(scaled_applied, weights)
        if iteration == 0:
            step_size = energy / curvature
            direction = smoothed
            direction_image = applied
            scaled_update = scaled_applied
            twice_update = applied_twice
        else:
            factor = energy / energy_old
            step_size = energy / (curvature - factor * energy / step_old)
            direction = smoothed + factor * direction
            direction_image = applied + factor * direction_image
            if not final_turn:
                scaled_update = scaled_applied + factor * scaled_update
                twice_update = applied_twice + factor * twice_update
        pressure = pressure + step_size * direction
        residual = residual - step_size * direction_image
        if not final_turn:
            smoothed = smoothed - step_size * scaled_update
            applied = applied - step_size * twice_update
        energy_old = energy
        step_old = step_size
    return (pressure, residual / diagonal)


def solution(mesh):
    return jax.shard_map(
        on_device,
        mesh=mesh,
        in_specs=(P("gz", "gx", "gy"), P("gz", "gx", "gy")),
        out_specs=(P("gz", "gx", "gy"), P("gz", "gx", "gy")),
        check_vma=False,
    )
```

profile of v0, /device:TPU:0, one launch (start us, length us, event | category | flops | bytes accessed | tf_op | source)
XLA Modules:
  0.0 218.4 jit_solution(12359695470842941293)
XLA Ops:
  0.6 0.8 fusion.76
  1.4 3.1 %collective-permute-start = (s32[8,1,128]{2,1,0:T(1,128)S(1)}, s32[8,1,128]{2,1,0:T(1,128)S(1)}, u32[]{:S(2)}, u32[]{:S(2)}) collective-permute-start(s32[8,1,128]{2,1,0:T(1,128)S(1)} %get-tuple-element.48), channel_id=1, source_target_pairs={{0,8},{8,16},{16,24},{24,0},{1,9},{9,17},{17,25},{25,1},{2,10},{10... | collective-permute-start | bytes 12296 | tf_op jit(solution)/shard_map/ppermute | solution.py:18
  4.5 2.1 collective-permute-start.1
  6.6 1.6 collective-permute-done
  8.1 1.0 pad_add_fusion
  9.1 0.1 fusion.73
  9.3 0.1 collective-permute-start.2
  9.3 1.7 collective-permute-start.3
  11.1 5.6 %collective-permute-done.2 = s32[8,66,1]{2,1,0:T(8,128)S(1)} collective-permute-done((s32[8,66,1]{2,1,0:T(8,128)S(1)}, s32[8,66,1]{2,1,0:T(8,128)S(1)}, u32[]{:S(2)}, u32[]{:S(2)}) %collective-permute-start.2) | collective-permute-done | bytes 2144 | tf_op jit(solution)/shard_map/ppermute | solution.py:18
  16.7 1.2 collective-permute-done.3
  17.8 0.1 pad_add_fusion.5
  18.0 1.6 collective-permute-start.4
  19.5 0.5 collective-permute-start.5
  20.0 2.9 %collective-permute-done.4 = s32[1,66,130]{2,1,0:T(8,128)S(1)} collective-permute-done((s32[1,66,130]{2,1,0:T(8,128)S(1)}, s32[1,66,130]{2,1,0:T(8,128)S(1)}, u32[]{:S(2)}, u32[]{:S(2)}) %collective-permute-start.4) | collective-permute-done | bytes 34352 | tf_op jit(solution)/shard_map/ppermute | solution.py:18
  23.0 1.4 collective-permute-done.5
  24.4 0.3 fusion.1
  24.8 0.5 fusion.61
  25.3 1.6 collective-permute-start.6
  26.9 2.4 %collective-permute-start.7 = (bf16[8,1,128]{2,1,0:T(2,128)(2,1)S(1)}, bf16[8,1,128]{2,1,0:T(2,128)(2,1)S(1)}, u32[]{:S(2)}, u32[]{:S(2)}) collective-permute-start(bf16[8,1,128]{2,1,0:T(2,128)(2,1)S(1)} %get-tuple-element.53), channel_id=1, source_target_pairs={{8,0},{16,8},{24,16},{0,24},{9,1},{17,9},{25,17},{1,25},{10,2},{18... | collective-permute-start | bytes 6152 | tf_op jit(solution)/shard_map/ppermute | solution.py:20
  29.2 1.5 collective-permute-done.6
  30.8 0.1 fusion.77
  30.9 0.1 collective-permute-start.8
  31.0 1.7 collective-permute-start.9
  32.7 2.8 %collective-permute-done.8 = bf16[8,66,1]{2,1,0:T(8,128)(2,1)S(1)} collective-permute-done((bf16[8,66,1]{2,1,0:T(8,128)(2,1)S(1)}, bf16[8,66,1]{2,1,0:T(8,128)(2,1)S(1)}, u32[]{:S(2)}, u32[]{:S(2)}) %collective-permute-start.8) | collective-permute-done | bytes 1088 | tf_op jit(solution)/shard_map/ppermute | solution.py:18
  35.5 0.8 collective-permute-done.9
  36.3 0.1 pad_maximum_fusion.53
  36.4 1.6 collective-permute-start.10
  38.0 0.5 collective-permute-start.11
  38.5 2.3 %collective-permute-done.10 = bf16[1,66,130]{2,1,0:T(8,128)(2,1)S(1)} collective-permute-done((bf16[1,66,130]{2,1,0:T(8,128)(2,1)S(1)}, bf16[1,66,130]{2,1,0:T(8,128)(2,1)S(1)}, u32[]{:S(2)}, u32[]{:S(2)}) %collective-permute-start.10) | collective-permute-done | bytes 17192 | tf_op jit(solution)/shard_map/ppermute | solution.py:18
  40.8 1.3 collective-permute-done.11
  42.1 0.2 maximum_convert_fusion
  42.4 1.1 multiply_reduce_fusion.4
  43.5 1.2 collective-permute-start.12
  44.7 2.8 %collective-permute-start.13 = (f32[8,1,128]{2,1,0:T(1,128)S(1)}, f32[8,1,128]{2,1,0:T(1,128)S(1)}, u32[]{:S(2)}, u32[]{:S(2)}) collective-permute-start(f32[8,1,128]{2,1,0:T(1,128)S(1)} %get-tuple-element.47), channel_id=1, source_target_pairs={{8,0},{16,8},{24,16},{0,24},{9,1},{17,9},{25,17},{1,25},{10,2},{18... | collective-permute-start | bytes 12296 | tf_op jit(solution)/shard_map/ppermute | solution.py:20
  47.5 1.5 collective-permute-done.12
  49.1 0.1 fusion.72
  49.2 0.1 collective-permute-start.14
  49.3 1.7 collective-permute-start.15
  51.0 5.7 %collective-permute-done.14 = f32[8,66,1]{2,1,0:T(8,128)S(1)} collective-permute-done((f32[8,66,1]{2,1,0:T(8,128)S(1)}, f32[8,66,1]{2,1,0:T(8,128)S(1)}, u32[]{:S(2)}, u32[]{:S(2)}) %collective-permute-start.14) | collective-permute-done | bytes 2144 | tf_op jit(solution)/shard_map/ppermute | solution.py:18
  56.8 0.9 collective-permute-done.15
  57.6 0.1 pad_maximum_fusion.48
  57.8 0.6 copy-done.4
  58.3 0.8 collective-permute-start.16
  59.2 1.2 collective-permute-start.17
  60.4 40.0 %all-reduce.2 = (f32[]{:T(128)}, f32[]{:T(128)}) all-reduce(f32[]{:T(128)} %get-tuple-element.5, f32[]{:T(128)} %get-tuple-element.4), channel_id=1, replica_groups=mesh['gx'=4,'gy'=4,'gz'=2] {'gx','gy','gz'}, use_global_device_ids=true, to_apply=%region_1.0 | all-reduce | flops 2 | bytes 16 | tf_op jit(solution)/shard_map/psum | solution.py:51
  101.7 1.5 fusion.60
  103.2 1.9 collective-permute-start.18
  105.1 2.0 collective-permute-start.19
  107.1 1.6 collective-permute-done.18
  108.7 0.1 collective-permute-done.19
  108.8 0.1 fusion.71
  109.0 1.7 collective-permute-start.21
  110.7 5.0 %collective-permute-done.20 = f32[8,66,1]{2,1,0:T(8,128)S(1)} collective-permute-done((f32[8,66,1]{2,1,0:T(8,128)S(1)}, f32[8,66,1]{2,1,0:T(8,128)S(1)}, u32[]{:S(2)}, u32[]{:S(2)}) %collective-permute-start.20) | collective-permute-done | bytes 2144 | tf_op jit(solution)/shard_map/ppermute | solution.py:18
  115.7 2.4 %collective-permute-done.21 = f32[8,66,1]{2,1,0:T(8,128)S(1)} collective-permute-done((f32[8,66,1]{2,1,0:T(8,128)S(1)}, f32[8,66,1]{2,1,0:T(8,128)S(1)}, u32[]{:S(2)}, u32[]{:S(2)}) %collective-permute-start.21) | collective-permute-done | bytes 2144 | tf_op jit(solution)/shard_map/ppermute | solution.py:20
  118.1 0.1 pad_maximum_fusion.43
  118.2 0.6 copy-done.3
  118.8 1.5 collective-permute-start.22
  120.3 0.6 collective-permute-start.23
  120.8 0.8 multiply_reduce_fusion.2
  121.6 40.3 %all-reduce.1 = (f32[]{:T(128)}, f32[]{:T(128)}) all-reduce(f32[]{:T(128)} %get-tuple-element.3, f32[]{:T(128)} %get-tuple-element.2), channel_id=1, replica_groups=mesh['gx'=4,'gy'=4,'gz'=2] {'gx','gy','gz'}, use_global_device_ids=true, to_apply=%region_5.0 | all-reduce | flops 2 | bytes 16 | tf_op jit(solution)/shard_map/psum | solution.py:51
  166.5 0.6 copy-done.5
  167.2 3.3 %multiply_reduce_fusion = (f32[]{:T(128)}, f32[]{:T(128)}, f32[8,64,128]{2,1,0:T(8,128)S(1)}, f32[8,64,128]{2,1,0:T(8,128)}) fusion(f32[8,64,128]{2,1,0:T(8,128)S(1)} %get-tuple-element.18, f32[8,64,128]{2,1,0:T(8,128)S(1)} %get-tuple-element.19, f32[]{:T(128)S(6)} %div.60, f32[8,64,128]{2,1,0:T(8,128)S(1)} %get-tuple-element.17, f32[]{:T(128)S(6)} %div.58, ...), kind=kLoop, calls=%fused_computation.114 | loop fusion | flops 3997694 | bytes 3882164 | tf_op jit(solution)/shard_map/reduce_sum | solution.py:51
  170.4 42.1 %all-reduce = (f32[]{:T(128)}, f32[]{:T(128)}) all-reduce(f32[]{:T(128)} %get-tuple-element.7, f32[]{:T(128)} %get-tuple-element.6), channel_id=1, replica_groups=mesh['gx'=4,'gy'=4,'gz'=2] {'gx','gy','gz'}, use_global_device_ids=true, to_apply=%region_9.0 | all-reduce | flops 2 | bytes 16 | tf_op jit(solution)/shard_map/psum | solution.py:51
  216.4 2.0 subtract_divide_fusion
  (24 shorter events, 0.3 us)
Async XLA Ops:
  1.4 6.7 %collective-permute-start = (s32[8,1,128]{2,1,0:T(1,128)S(1)}, s32[8,1,128]{2,1,0:T(1,128)S(1)}, u32[]{:S(2)}, u32[]{:S(2)}) collective-permute-start(s32[8,1,128]{2,1,0:T(1,128)S(1)} %get-tuple-element.48), channel_id=1, source_target_pairs={{0,8},{8,16},{16,24},{24,0},{1,9},{9,17},{17,25},{25,1},{2,10},{10... | collective-permute-start | bytes 12296 | tf_op jit(solution)/shard_map/ppermute | solution.py:18
  4.5 3.7 %collective-permute-start.1 = (s32[8,1,128]{2,1,0:T(1,128)S(1)}, s32[8,1,128]{2,1,0:T(1,128)S(1)}, u32[]{:S(2)}, u32[]{:S(2)}) collective-permute-start(s32[8,1,128]{2,1,0:T(1,128)S(1)} %get-tuple-element.49), channel_id=1, source_target_pairs={{8,0},{16,8},{24,16},{0,24},{9,1},{17,9},{25,17},{1,25},{10,2},{18... | collective-permute-start | bytes 12296 | tf_op jit(solution)/shard_map/ppermute | solution.py:20
  9.1 8.7 %copy-start.1 = (s32[8,64,128]{2,1,0:T(8,128)S(1)}, s32[8,64,128]{2,1,0:T(8,128)}, u32[]{:S(2)}) copy-start(s32[8,64,128]{2,1,0:T(8,128)} %param.3) | copy-start | bytes 786436
  9.3 7.4 %collective-permute-start.2 = (s32[8,66,1]{2,1,0:T(8,128)S(1)}, s32[8,66,1]{2,1,0:T(8,128)S(1)}, u32[]{:S(2)}, u32[]{:S(2)}) collective-permute-start(s32[8,66,1]{2,1,0:T(8,128)S(1)} %get-tuple-element.40), channel_id=1, source_target_pairs={{0,2},{2,4},{4,6},{6,0},{1,3},{3,5},{5,7},{7,1},{8,10},{10,12},{12... | collective-permute-start | bytes 6344 | tf_op jit(solution)/shard_map/ppermute | solution.py:18
  9.3 8.5 %collective-permute-start.3 = (s32[8,66,1]{2,1,0:T(8,128)S(1)}, s32[8,66,1]{2,1,0:T(8,128)S(1)}, u32[]{:S(2)}, u32[]{:S(2)}) collective-permute-start(s32[8,66,1]{2,1,0:T(8,128)S(1)} %get-tuple-element.41), channel_id=1, source_target_pairs={{2,0},{4,2},{6,4},{0,6},{3,1},{5,3},{7,5},{1,7},{10,8},{12,10},{14... | collective-permute-start | bytes 6344 | tf_op jit(solution)/shard_map/ppermute | solution.py:20
  18.0 5.0 %collective-permute-start.4 = (s32[1,66,130]{2,1,0:T(8,128)S(1)}, s32[1,66,130]{2,1,0:T(8,128)S(1)}, u32[]{:S(2)}, u32[]{:S(2)}) collective-permute-start(s32[1,66,130]{2,1,0:T(8,128)S(1)} %get-tuple-element.32), channel_id=1, source_target_pairs={{0,1},{1,0},{2,3},{3,2},{4,5},{5,4},{6,7},{7,6},{8,9},{9,8},{10,11... | collective-permute-start | bytes 102968 | tf_op jit(solution)/shard_map/ppermute | solution.py:18
  19.5 5.2 %copy-start = (bf16[8,64,128]{2,1,0:T(8,128)(2,1)S(1)}, bf16[8,64,128]{2,1,0:T(8,128)(2,1)}, u32[]{:S(2)}) copy-start(bf16[8,64,128]{2,1,0:T(8,128)(2,1)} %param.2) | copy-start | bytes 393220
  19.5 4.9 %collective-permute-start.5 = (s32[1,66,130]{2,1,0:T(8,128)S(1)}, s32[1,66,130]{2,1,0:T(8,128)S(1)}, u32[]{:S(2)}, u32[]{:S(2)}) collective-permute-start(s32[1,66,130]{2,1,0:T(8,128)S(1)} %get-tuple-element.33), channel_id=1, source_target_pairs={{1,0},{0,1},{3,2},{2,3},{5,4},{4,5},{7,6},{6,7},{9,8},{8,9},{11,10... | collective-permute-start | bytes 102968 | tf_op jit(solution)/shard_map/ppermute | solution.py:20
  25.3 5.5 %collective-permute-start.6 = (bf16[8,1,128]{2,1,0:T(2,128)(2,1)S(1)}, bf16[8,1,128]{2,1,0:T(2,128)(2,1)S(1)}, u32[]{:S(2)}, u32[]{:S(2)}) collective-permute-start(bf16[8,1,128]{2,1,0:T(2,128)(2,1)S(1)} %get-tuple-element.52), channel_id=1, source_target_pairs={{0,8},{8,16},{16,24},{24,0},{1,9},{9,17},{17,25},{25,1},{2,10},{10... | collective-permute-start | bytes 6152 | tf_op jit(solution)/shard_map/ppermute | solution.py:18
  26.9 3.9 %collective-permute-start.7 = (bf16[8,1,128]{2,1,0:T(2,128)(2,1)S(1)}, bf16[8,1,128]{2,1,0:T(2,128)(2,1)S(1)}, u32[]{:S(2)}, u32[]{:S(2)}) collective-permute-start(bf16[8,1,128]{2,1,0:T(2,128)(2,1)S(1)} %get-tuple-element.53), channel_id=1, source_target_pairs={{8,0},{16,8},{24,16},{0,24},{9,1},{17,9},{25,17},{1,25},{10,2},{18... | collective-permute-start | bytes 6152 | tf_op jit(solution)/shard_map/ppermute | solution.py:20
  30.9 4.6 %collective-permute-start.8 = (bf16[8,66,1]{2,1,0:T(8,128)(2,1)S(1)}, bf16[8,66,1]{2,1,0:T(8,128)(2,1)S(1)}, u32[]{:S(2)}, u32[]{:S(2)}) collective-permute-start(bf16[8,66,1]{2,1,0:T(8,128)(2,1)S(1)} %get-tuple-element.50), channel_id=1, source_target_pairs={{0,2},{2,4},{4,6},{6,0},{1,3},{3,5},{5,7},{7,1},{8,10},{10,12},{12... | collective-permute-start | bytes 3176 | tf_op jit(solution)/shard_map/ppermute | solution.py:18
  31.0 5.3 %collective-permute-start.9 = (bf16[8,66,1]{2,1,0:T(8,128)(2,1)S(1)}, bf16[8,66,1]{2,1,0:T(8,128)(2,1)S(1)}, u32[]{:S(2)}, u32[]{:S(2)}) collective-permute-start(bf16[8,66,1]{2,1,0:T(8,128)(2,1)S(1)} %get-tuple-element.51), channel_id=1, source_target_pairs={{2,0},{4,2},{6,4},{0,6},{3,1},{5,3},{7,5},{1,7},{10,8},{12,10},{14... | collective-permute-start | bytes 3176 | tf_op jit(solution)/shard_map/ppermute | solution.py:20
  36.4 4.4 %collective-permute-start.10 = (bf16[1,66,130]{2,1,0:T(8,128)(2,1)S(1)}, bf16[1,66,130]{2,1,0:T(8,128)(2,1)S(1)}, u32[]{:S(2)}, u32[]{:S(2)}) collective-permute-start(bf16[1,66,130]{2,1,0:T(8,128)(2,1)S(1)} %get-tuple-element.34), channel_id=1, source_target_pairs={{0,1},{1,0},{2,3},{3,2},{4,5},{5,4},{6,7},{7,6},{8,9},{9,8},{10,11... | collective-permute-start | bytes 51488 | tf_op jit(solution)/shard_map/ppermute | solution.py:18
  38.0 4.1 %collective-permute-start.11 = (bf16[1,66,130]{2,1,0:T(8,128)(2,1)S(1)}, bf16[1,66,130]{2,1,0:T(8,128)(2,1)S(1)}, u32[]{:S(2)}, u32[]{:S(2)}) collective-permute-start(bf16[1,66,130]{2,1,0:T(8,128)(2,1)S(1)} %get-tuple-element.35), channel_id=1, source_target_pairs={{1,0},{0,1},{3,2},{2,3},{5,4},{4,5},{7,6},{6,7},{9,8},{8,9},{11,10... | collective-permute-start | bytes 51488 | tf_op jit(solution)/shard_map/ppermute | solution.py:20
  43.5 5.5 %collective-permute-start.12 = (f32[8,1,128]{2,1,0:T(1,128)S(1)}, f32[8,1,128]{2,1,0:T(1,128)S(1)}, u32[]{:S(2)}, u32[]{:S(2)}) collective-permute-start(f32[8,1,128]{2,1,0:T(1,128)S(1)} %get-tuple-element.46), channel_id=1, source_target_pairs={{0,8},{8,16},{16,24},{24,0},{1,9},{9,17},{17,25},{25,1},{2,10},{10... | collective-permute-start | bytes 12296 | tf_op jit(solution)/shard_map/ppermute | solution.py:18
  44.7 4.3 %collective-permute-start.13 = (f32[8,1,128]{2,1,0:T(1,128)S(1)}, f32[8,1,128]{2,1,0:T(1,128)S(1)}, u32[]{:S(2)}, u32[]{:S(2)}) collective-permute-start(f32[8,1,128]{2,1,0:T(1,128)S(1)} %get-tuple-element.47), channel_id=1, source_target_pairs={{8,0},{16,8},{24,16},{0,24},{9,1},{17,9},{25,17},{1,25},{10,2},{18... | collective-permute-start | bytes 12296 | tf_op jit(solution)/shard_map/ppermute | solution.py:20
  49.2 7.5 %collective-permute-start.14 = (f32[8,66,1]{2,1,0:T(8,128)S(1)}, f32[8,66,1]{2,1,0:T(8,128)S(1)}, u32[]{:S(2)}, u32[]{:S(2)}) collective-permute-start(f32[8,66,1]{2,1,0:T(8,128)S(1)} %get-tuple-element.38), channel_id=1, source_target_pairs={{0,2},{2,4},{4,6},{6,0},{1,3},{3,5},{5,7},{7,1},{8,10},{10,12},{12... | collective-permute-start | bytes 6344 | tf_op jit(solution)/shard_map/ppermute | solution.py:18
  49.3 8.3 %collective-permute-start.15 = (f32[8,66,1]{2,1,0:T(8,128)S(1)}, f32[8,66,1]{2,1,0:T(8,128)S(1)}, u32[]{:S(2)}, u32[]{:S(2)}) collective-permute-start(f32[8,66,1]{2,1,0:T(8,128)S(1)} %get-tuple-element.39), channel_id=1, source_target_pairs={{2,0},{4,2},{6,4},{0,6},{3,1},{5,3},{7,5},{1,7},{10,8},{12,10},{14... | collective-permute-start | bytes 6344 | tf_op jit(solution)/shard_map/ppermute | solution.py:20
  57.6 0.7 copy-start.4
  58.3 43.4 %collective-permute-start.16 = (f32[1,66,130]{2,1,0:T(8,128)S(1)}, f32[1,66,130]{2,1,0:T(8,128)S(1)}, u32[]{:S(2)}, u32[]{:S(2)}) collective-permute-start(f32[1,66,130]{2,1,0:T(8,128)S(1)} %get-tuple-element.30), channel_id=1, source_target_pairs={{0,1},{1,0},{2,3},{3,2},{4,5},{5,4},{6,7},{7,6},{8,9},{9,8},{10,11... | collective-permute-start | bytes 102968 | tf_op jit(solution)/shard_map/ppermute | solution.py:18
  59.2 42.6 %collective-permute-start.17 = (f32[1,66,130]{2,1,0:T(8,128)S(1)}, f32[1,66,130]{2,1,0:T(8,128)S(1)}, u32[]{:S(2)}, u32[]{:S(2)}) collective-permute-start(f32[1,66,130]{2,1,0:T(8,128)S(1)} %get-tuple-element.31), channel_id=1, source_target_pairs={{1,0},{0,1},{3,2},{2,3},{5,4},{4,5},{7,6},{6,7},{9,8},{8,9},{11,10... | collective-permute-start | bytes 102968 | tf_op jit(solution)/shard_map/ppermute | solution.py:20
  103.2 5.5 %collective-permute-start.18 = (f32[8,1,128]{2,1,0:T(1,128)S(1)}, f32[8,1,128]{2,1,0:T(1,128)S(1)}, u32[]{:S(2)}, u32[]{:S(2)}) collective-permute-start(f32[8,1,128]{2,1,0:T(1,128)S(1)} %get-tuple-element.44), channel_id=1, source_target_pairs={{0,8},{8,16},{16,24},{24,0},{1,9},{9,17},{17,25},{25,1},{2,10},{10... | collective-permute-start | bytes 12296 | tf_op jit(solution)/shard_map/ppermute | solution.py:18
  105.1 3.6 %collective-permute-start.19 = (f32[8,1,128]{2,1,0:T(1,128)S(1)}, f32[8,1,128]{2,1,0:T(1,128)S(1)}, u32[]{:S(2)}, u32[]{:S(2)}) collective-permute-start(f32[8,1,128]{2,1,0:T(1,128)S(1)} %get-tuple-element.45), channel_id=1, source_target_pairs={{8,0},{16,8},{24,16},{0,24},{9,1},{17,9},{25,17},{1,25},{10,2},{18... | collective-permute-start | bytes 12296 | tf_op jit(solution)/shard_map/ppermute | solution.py:20
  108.9 6.8 %collective-permute-start.20 = (f32[8,66,1]{2,1,0:T(8,128)S(1)}, f32[8,66,1]{2,1,0:T(8,128)S(1)}, u32[]{:S(2)}, u32[]{:S(2)}) collective-permute-start(f32[8,66,1]{2,1,0:T(8,128)S(1)} %get-tuple-element.36), channel_id=1, source_target_pairs={{0,2},{2,4},{4,6},{6,0},{1,3},{3,5},{5,7},{7,1},{8,10},{10,12},{12... | collective-permute-start | bytes 6344 | tf_op jit(solution)/shard_map/ppermute | solution.py:18
  109.0 9.1 %collective-permute-start.21 = (f32[8,66,1]{2,1,0:T(8,128)S(1)}, f32[8,66,1]{2,1,0:T(8,128)S(1)}, u32[]{:S(2)}, u32[]{:S(2)}) collective-permute-start(f32[8,66,1]{2,1,0:T(8,128)S(1)} %get-tuple-element.37), channel_id=1, source_target_pairs={{2,0},{4,2},{6,4},{0,6},{3,1},{5,3},{7,5},{1,7},{10,8},{12,10},{14... | collective-permute-start | bytes 6344 | tf_op jit(solution)/shard_map/ppermute | solution.py:20
  115.7 2.5 %copy-start.2 = (f32[8,66,1]{2,1,0:T(8,128)}, f32[8,66,1]{2,1,0:T(8,128)S(1)}, u32[]{:S(2)}) copy-start(f32[8,66,1]{2,1,0:T(8,128)S(1)} %collective-permute-done.20) | copy-start | bytes 6340
  118.1 0.7 copy-start.3
  118.8 47.7 %collective-permute-start.22 = (f32[1,66,130]{2,1,0:T(8,128)S(1)}, f32[1,66,130]{2,1,0:T(8,128)S(1)}, u32[]{:S(2)}, u32[]{:S(2)}) collective-permute-start(f32[1,66,130]{2,1,0:T(8,128)S(1)} %get-tuple-element.28), channel_id=1, source_target_pairs={{0,1},{1,0},{2,3},{3,2},{4,5},{5,4},{6,7},{7,6},{8,9},{9,8},{10,11... | collective-permute-start | bytes 102968 | tf_op jit(solution)/shard_map/ppermute | solution.py:18
  120.3 46.3 %collective-permute-start.23 = (f32[1,66,130]{2,1,0:T(8,128)S(1)}, f32[1,66,130]{2,1,0:T(8,128)}, u32[]{:S(2)}, u32[]{:S(2)}) collective-permute-start(f32[1,66,130]{2,1,0:T(8,128)S(1)} %get-tuple-element.29), channel_id=1, source_target_pairs={{1,0},{0,1},{3,2},{2,3},{5,4},{4,5},{7,6},{6,7},{9,8},{8,9},{11,10... | collective-permute-start | bytes 102968 | tf_op jit(solution)/shard_map/ppermute | solution.py:20
  166.5 0.6 copy-start.5
where the time goes:
time: 219 us; the launch traced here: 218 us
  blocking collectives  122 us (56%)
  waiting for transfers between devices  38.5 us (18%)
  starting transfers between devices  32.4 us (15%)
  other arithmetic  11.3 us (5%)
  between operations  10.7 us (5%)
  local copies, waits for them, and re-layouts  3.12 us (1%)
    psum x3, blocking collectives, products(): lax.psum((jnp.sum(first * second), jnp.sum(third * fourth)), ('gx', 'gy',...  122 us
    ppermute x12, waiting for transfers between devices, padded_2(): lax.ppermute(tail, axis, [(i, (i + 1) % count) for i in range(count)])  30.6 us
    ppermute x12, starting transfers between devices, padded_2(): lax.ppermute(head, axis, [((i + 1) % count, i) for i in range(count)])  19 us
    ppermute x12, starting transfers between devices, padded_2(): lax.ppermute(tail, axis, [(i, (i + 1) % count) for i in range(count)])  13.4 us
    ppermute x12, waiting for transfers between devices, padded_2(): lax.ppermute(head, axis, [((i + 1) % count, i) for i in range(count)])  7.98 us
    reduce_sum x3, other arithmetic, products(): jnp.sum(third * fourth)  5.16 us
  transfers between devices with their start and end apart: 24, of which 17 were waited for; matrix products, arithmetic and copies ran while one was open for 0% of the time, Pallas kernels for 0%

commit v1 on v0

--- a/solution.py
+++ b/solution.py
@@ -48,7 +48,9 @@
 
 
 def products(first, second, third, fourth):
-    return lax.psum((jnp.sum(first * second), jnp.sum(third * fourth)), ("gx", "gy", "gz"))
+    return lax.psum(
+        lax.psum((jnp.sum(first * second), jnp.sum(third * fourth)), ("gy", "gz")), "gx"
+    )
 
 
 def build_weights(density_padded):

time: 219 us -> 172 us (0.79)
  blocking collectives: 122 us -> 76.2 us
    psum x3 -> x6, blocking collectives: 122 us -> 76.2 us  [the longest x3 41.4 us: products(): lax.psum((jnp.sum(first * second), jnp.sum(third * fourth)), ('gy', 'gz'))]
    ppermute x12, starting transfers between devices: 13.4 us -> 10.9 us  [padded_2(): lax.ppermute(tail, axis, [(i, (i + 1) % count) for i in range(count)])]
    ppermute x12, starting transfers between devices: 19 us -> 21.5 us  [padded_2(): lax.ppermute(head, axis, [((i + 1) % count, i) for i in range(count)])]
    ppermute x12, waiting for transfers between devices: 7.98 us -> 5.54 us  [padded_2(): lax.ppermute(head, axis, [((i + 1) % count, i) for i in range(count)])]
  transfers between devices with their start and end apart: 24 -> 24, of which waited for: 17 -> 15; matrix products, arithmetic and copies ran while one was open for 0% -> 0% of each run, Pallas kernels for 0% -> 0%
where the time goes in v1:
time: 172 us
  blocking collectives  76.2 us (44%)
  waiting for transfers between devices  37.6 us (22%)
  starting transfers between devices  32.4 us (19%)
  other arithmetic  11.4 us (7%)
  between operations  11 us (6%)
  local copies, waits for them, and re-layouts  3.24 us (2%)
    psum x3, blocking collectives, products(): lax.psum((jnp.sum(first * second), jnp.sum(third * fourth)), ('gy', 'gz'))  41.4 us
    psum x3, blocking collectives, products(): lax.psum(lax.psum((jnp.sum(first * second), jnp.sum(third * fourth)), ('g...  34.8 us
    ppermute x12, waiting for transfers between devices, padded_2(): lax.ppermute(tail, axis, [(i, (i + 1) % count) for i in range(count)])  32.1 us
    ppermute x12, starting transfers between devices, padded_2(): lax.ppermute(head, axis, [((i + 1) % count, i) for i in range(count)])  21.5 us
    ppermute x12, starting transfers between devices, padded_2(): lax.ppermute(tail, axis, [(i, (i + 1) % count) for i in range(count)])  10.9 us
    ppermute x12, waiting for transfers between devices, padded_2(): lax.ppermute(head, axis, [((i + 1) % count, i) for i in range(count)])  5.54 us
    reduce_sum x3, other arithmetic, products(): jnp.sum(third * fourth)  5.21 us
  transfers between devices with their start and end apart: 24, of which 15 were waited for; matrix products, arithmetic and copies ran while one was open for 0% of the time, Pallas kernels for 0%

profile of v1, /device:TPU:0, one launch (start us, length us, event | category | flops | bytes accessed | tf_op | source)
XLA Modules:
  0.0 171.8 jit_solution(4114740684292452823)
XLA Ops:
  0.6 0.8 fusion.76
  1.4 3.1 %collective-permute-start = (s32[8,1,128]{2,1,0:T(1,128)S(1)}, s32[8,1,128]{2,1,0:T(1,128)S(1)}, u32[]{:S(2)}, u32[]{:S(2)}) collective-permute-start(s32[8,1,128]{2,1,0:T(1,128)S(1)} %get-tuple-element.54), channel_id=1, source_target_pairs={{0,8},{8,16},{16,24},{24,0},{1,9},{9,17},{17,25},{25,1},{2,10},{10... | collective-permute-start | bytes 12296 | tf_op jit(solution)/shard_map/ppermute | solution.py:18
  4.5 2.1 %collective-permute-start.1 = (s32[8,1,128]{2,1,0:T(1,128)S(1)}, s32[8,1,128]{2,1,0:T(1,128)S(1)}, u32[]{:S(2)}, u32[]{:S(2)}) collective-permute-start(s32[8,1,128]{2,1,0:T(1,128)S(1)} %get-tuple-element.55), channel_id=1, source_target_pairs={{8,0},{16,8},{24,16},{0,24},{9,1},{17,9},{25,17},{1,25},{10,2},{18... | collective-permute-start | bytes 12296 | tf_op jit(solution)/shard_map/ppermute | solution.py:20
  6.6 1.6 collective-permute-done
  8.1 1.0 pad_add_fusion
  9.1 0.1 fusion.73
  9.3 0.1 collective-permute-start.2
  9.3 1.7 %collective-permute-start.3 = (s32[8,66,1]{2,1,0:T(8,128)S(1)}, s32[8,66,1]{2,1,0:T(8,128)S(1)}, u32[]{:S(2)}, u32[]{:S(2)}) collective-permute-start(s32[8,66,1]{2,1,0:T(8,128)S(1)} %get-tuple-element.47), channel_id=1, source_target_pairs={{2,0},{4,2},{6,4},{0,6},{3,1},{5,3},{7,5},{1,7},{10,8},{12,10},{14... | collective-permute-start | bytes 6344 | tf_op jit(solution)/shard_map/ppermute | solution.py:20
  11.1 5.6 %collective-permute-done.2 = s32[8,66,1]{2,1,0:T(8,128)S(1)} collective-permute-done((s32[8,66,1]{2,1,0:T(8,128)S(1)}, s32[8,66,1]{2,1,0:T(8,128)S(1)}, u32[]{:S(2)}, u32[]{:S(2)}) %collective-permute-start.2) | collective-permute-done | bytes 2144 | tf_op jit(solution)/shard_map/ppermute | solution.py:18
  16.7 1.2 collective-permute-done.3
  17.8 0.1 pad_add_fusion.5
  18.0 1.6 collective-permute-start.4
  19.5 0.5 collective-permute-start.5
  20.0 2.9 %collective-permute-done.4 = s32[1,66,130]{2,1,0:T(8,128)S(1)} collective-permute-done((s32[1,66,130]{2,1,0:T(8,128)S(1)}, s32[1,66,130]{2,1,0:T(8,128)S(1)}, u32[]{:S(2)}, u32[]{:S(2)}) %collective-permute-start.4) | collective-permute-done | bytes 34352 | tf_op jit(solution)/shard_map/ppermute | solution.py:18
  23.0 1.4 collective-permute-done.5
  24.4 0.3 fusion.1
  24.8 0.5 fusion.61
  25.3 1.6 collective-permute-start.6
  26.9 2.4 %collective-permute-start.7 = (bf16[8,1,128]{2,1,0:T(2,128)(2,1)S(1)}, bf16[8,1,128]{2,1,0:T(2,128)(2,1)S(1)}, u32[]{:S(2)}, u32[]{:S(2)}) collective-permute-start(bf16[8,1,128]{2,1,0:T(2,128)(2,1)S(1)} %get-tuple-element.59), channel_id=1, source_target_pairs={{8,0},{16,8},{24,16},{0,24},{9,1},{17,9},{25,17},{1,25},{10,2},{18... | collective-permute-start | bytes 6152 | tf_op jit(solution)/shard_map/ppermute | solution.py:20
  29.2 1.5 collective-permute-done.6
  30.8 0.1 fusion.77
  31.0 1.7 %collective-permute-start.9 = (bf16[8,66,1]{2,1,0:T(8,128)(2,1)S(1)}, bf16[8,66,1]{2,1,0:T(8,128)(2,1)S(1)}, u32[]{:S(2)}, u32[]{:S(2)}) collective-permute-start(bf16[8,66,1]{2,1,0:T(8,128)(2,1)S(1)} %get-tuple-element.57), channel_id=1, source_target_pairs={{2,0},{4,2},{6,4},{0,6},{3,1},{5,3},{7,5},{1,7},{10,8},{12,10},{14... | collective-permute-start | bytes 3176 | tf_op jit(solution)/shard_map/ppermute | solution.py:20
  32.7 2.8 %collective-permute-done.8 = bf16[8,66,1]{2,1,0:T(8,128)(2,1)S(1)} collective-permute-done((bf16[8,66,1]{2,1,0:T(8,128)(2,1)S(1)}, bf16[8,66,1]{2,1,0:T(8,128)(2,1)S(1)}, u32[]{:S(2)}, u32[]{:S(2)}) %collective-permute-start.8) | collective-permute-done | bytes 1088 | tf_op jit(solution)/shard_map/ppermute | solution.py:18
  35.5 0.8 collective-permute-done.9
  36.3 0.1 pad_maximum_fusion.53
  36.4 1.6 collective-permute-start.10
  38.0 0.5 collective-permute-start.11
  38.5 2.3 %collective-permute-done.10 = bf16[1,66,130]{2,1,0:T(8,128)(2,1)S(1)} collective-permute-done((bf16[1,66,130]{2,1,0:T(8,128)(2,1)S(1)}, bf16[1,66,130]{2,1,0:T(8,128)(2,1)S(1)}, u32[]{:S(2)}, u32[]{:S(2)}) %collective-permute-start.10) | collective-permute-done | bytes 17192 | tf_op jit(solution)/shard_map/ppermute | solution.py:18
  40.8 1.3 collective-permute-done.11
  42.1 0.2 maximum_convert_fusion
  42.4 1.1 multiply_reduce_fusion.4
  43.5 1.2 collective-permute-start.12
  44.7 2.8 %collective-permute-start.13 = (f32[8,1,128]{2,1,0:T(1,128)S(1)}, f32[8,1,128]{2,1,0:T(1,128)S(1)}, u32[]{:S(2)}, u32[]{:S(2)}) collective-permute-start(f32[8,1,128]{2,1,0:T(1,128)S(1)} %get-tuple-element.53), channel_id=1, source_target_pairs={{8,0},{16,8},{24,16},{0,24},{9,1},{17,9},{25,17},{1,25},{10,2},{18... | collective-permute-start | bytes 12296 | tf_op jit(solution)/shard_map/ppermute | solution.py:20
  47.5 1.5 collective-permute-done.12
  49.1 0.1 fusion.72
  49.3 1.7 %collective-permute-start.15 = (f32[8,66,1]{2,1,0:T(8,128)S(1)}, f32[8,66,1]{2,1,0:T(8,128)S(1)}, u32[]{:S(2)}, u32[]{:S(2)}) collective-permute-start(f32[8,66,1]{2,1,0:T(8,128)S(1)} %get-tuple-element.45), channel_id=1, source_target_pairs={{2,0},{4,2},{6,4},{0,6},{3,1},{5,3},{7,5},{1,7},{10,8},{12,10},{14... | collective-permute-start | bytes 6344 | tf_op jit(solution)/shard_map/ppermute | solution.py:20
  51.0 5.7 %collective-permute-done.14 = f32[8,66,1]{2,1,0:T(8,128)S(1)} collective-permute-done((f32[8,66,1]{2,1,0:T(8,128)S(1)}, f32[8,66,1]{2,1,0:T(8,128)S(1)}, u32[]{:S(2)}, u32[]{:S(2)}) %collective-permute-start.14) | collective-permute-done | bytes 2144 | tf_op jit(solution)/shard_map/ppermute | solution.py:18
  56.8 0.9 collective-permute-done.15
  57.6 0.1 pad_maximum_fusion.48
  57.8 0.6 copy-done.4
  58.3 0.8 collective-permute-start.16
  59.2 1.2 collective-permute-start.17
  60.4 14.1 %all-reduce.2 = (f32[]{:T(128)}, f32[]{:T(128)}) all-reduce(f32[]{:T(128)} %get-tuple-element.5, f32[]{:T(128)} %get-tuple-element.4), channel_id=1, replica_groups=mesh['gx'=4,'gy'=4,'gz'=2] {'gy','gz'}, use_global_device_ids=true, to_apply=%region_1.0 | all-reduce | flops 2 | bytes 16 | tf_op jit(solution)/shard_map/psum | solution.py:52
  74.5 12.9 %all-reduce.5 = (f32[]{:T(128)}, f32[]{:T(128)}) all-reduce(f32[]{:T(128)} %get-tuple-element.12, f32[]{:T(128)} %get-tuple-element.13), channel_id=1, replica_groups=mesh['gx'=4,'gy'=4,'gz'=2] {'gx'}, use_global_device_ids=true, to_apply=%region_2.0 | all-reduce | flops 2 | bytes 16 | tf_op jit(solution)/shard_map/psum | solution.py:51
  88.7 1.5 fusion.60
  90.1 0.1 collective-permute-start.18
  90.2 3.8 %collective-permute-start.19 = (f32[8,1,128]{2,1,0:T(1,128)S(1)}, f32[8,1,128]{2,1,0:T(1,128)S(1)}, u32[]{:S(2)}, u32[]{:S(2)}) collective-permute-start(f32[8,1,128]{2,1,0:T(1,128)S(1)} %get-tuple-element.51), channel_id=1, source_target_pairs={{8,0},{16,8},{24,16},{0,24},{9,1},{17,9},{25,17},{1,25},{10,2},{18... | collective-permute-start | bytes 12296 | tf_op jit(solution)/shard_map/ppermute | solution.py:20
  94.0 1.6 collective-permute-done.18
  95.6 0.1 fusion.71
  95.9 1.7 %collective-permute-start.21 = (f32[8,66,1]{2,1,0:T(8,128)S(1)}, f32[8,66,1]{2,1,0:T(8,128)S(1)}, u32[]{:S(2)}, u32[]{:S(2)}) collective-permute-start(f32[8,66,1]{2,1,0:T(8,128)S(1)} %get-tuple-element.43), channel_id=1, source_target_pairs={{2,0},{4,2},{6,4},{0,6},{3,1},{5,3},{7,5},{1,7},{10,8},{12,10},{14... | collective-permute-start | bytes 6344 | tf_op jit(solution)/shard_map/ppermute | solution.py:20
  97.6 6.5 %collective-permute-done.20 = f32[8,66,1]{2,1,0:T(8,128)S(1)} collective-permute-done((f32[8,66,1]{2,1,0:T(8,128)S(1)}, f32[8,66,1]{2,1,0:T(8,128)S(1)}, u32[]{:S(2)}, u32[]{:S(2)}) %collective-permute-start.20) | collective-permute-done | bytes 2144 | tf_op jit(solution)/shard_map/ppermute | solution.py:18
  104.1 0.1 pad_maximum_fusion.43
  104.2 0.6 copy-done.2
  104.8 0.1 copy-done.3
  104.9 0.8 collective-permute-start.22
  105.7 1.3 collective-permute-start.23
  107.0 0.9 multiply_reduce_fusion.2
  107.8 14.0 %all-reduce.1 = (f32[]{:T(128)}, f32[]{:T(128)}) all-reduce(f32[]{:T(128)} %get-tuple-element.3, f32[]{:T(128)} %get-tuple-element.2), channel_id=1, replica_groups=mesh['gx'=4,'gy'=4,'gz'=2] {'gy','gz'}, use_global_device_ids=true, to_apply=%region_7.0 | all-reduce | flops 2 | bytes 16 | tf_op jit(solution)/shard_map/psum | solution.py:52
  121.8 12.9 %all-reduce.4 = (f32[]{:T(128)}, f32[]{:T(128)}) all-reduce(f32[]{:T(128)} %get-tuple-element.10, f32[]{:T(128)} %get-tuple-element.11), channel_id=1, replica_groups=mesh['gx'=4,'gy'=4,'gz'=2] {'gx'}, use_global_device_ids=true, to_apply=%region_8.0 | all-reduce | flops 2 | bytes 16 | tf_op jit(solution)/shard_map/psum | solution.py:51
  139.5 0.6 copy-done.5
  140.1 3.3 %multiply_reduce_fusion = (f32[]{:T(128)}, f32[]{:T(128)}, f32[8,64,128]{2,1,0:T(8,128)S(1)}, f32[8,64,128]{2,1,0:T(8,128)}) fusion(f32[8,64,128]{2,1,0:T(8,128)S(1)} %get-tuple-element.24, f32[8,64,128]{2,1,0:T(8,128)S(1)} %get-tuple-element.25, f32[]{:T(128)S(6)} %div.60, f32[8,64,128]{2,1,0:T(8,128)S(1)} %get-tuple-element.23, f32[]{:T(128)S(6)} %div.58, ...), kind=kLoop, calls=%fused_computation.114 | loop fusion | flops 3997694 | bytes 3882164 | tf_op jit(solution)/shard_map/reduce_sum | solution.py:52
  143.4 13.3 %all-reduce = (f32[]{:T(128)}, f32[]{:T(128)}) all-reduce(f32[]{:T(128)} %get-tuple-element.7, f32[]{:T(128)} %get-tuple-element.6), channel_id=1, replica_groups=mesh['gx'=4,'gy'=4,'gz'=2] {'gy','gz'}, use_global_device_ids=true, to_apply=%region_13.0 | all-reduce | flops 2 | bytes 16 | tf_op jit(solution)/shard_map/psum | solution.py:52
  156.7 9.1 %all-reduce.3 = (f32[]{:T(128)}, f32[]{:T(128)}) all-reduce(f32[]{:T(128)} %get-tuple-element.8, f32[]{:T(128)} %get-tuple-element.9), channel_id=1, replica_groups=mesh['gx'=4,'gy'=4,'gz'=2] {'gx'}, use_global_device_ids=true, to_apply=%region_14.0 | all-reduce | flops 2 | bytes 16 | tf_op jit(solution)/shard_map/psum | solution.py:51
  169.8 2.0 %subtract_divide_fusion = (f32[8,64,128]{2,1,0:T(8,128)}, f32[8,64,128]{2,1,0:T(8,128)}) fusion(f32[8,64,128]{2,1,0:T(8,128)S(1)} %get-tuple-element.27, f32[8,64,128]{2,1,0:T(8,128)S(1)} %get-tuple-element.20, f32[8,64,128]{2,1,0:T(8,128)S(1)} %get-tuple-element.24, f32[]{:T(128)S(6)} %div.64, f32[]{:T(128)S(6)} %div.66, f32[]{:T(128)S(6)} %div.62, ...), kind=kLoop, calls=%fused_computation.112 | loop fusion | flops 1638400 | bytes 2490388 | tf_op jit(solution)/shard_map/div | solution.py:113
  (27 shorter events, 0.4 us)
Async XLA Ops:
  1.4 6.7 %collective-permute-start = (s32[8,1,128]{2,1,0:T(1,128)S(1)}, s32[8,1,128]{2,1,0:T(1,128)S(1)}, u32[]{:S(2)}, u32[]{:S(2)}) collective-permute-start(s32[8,1,128]{2,1,0:T(1,128)S(1)} %get-tuple-element.54), channel_id=1, source_target_pairs={{0,8},{8,16},{16,24},{24,0},{1,9},{9,17},{17,25},{25,1},{2,10},{10... | collective-permute-start | bytes 12296 | tf_op jit(solution)/shard_map/ppermute | solution.py:18
  4.5 3.7 %collective-permute-start.1 = (s32[8,1,128]{2,1,0:T(1,128)S(1)}, s32[8,1,128]{2,1,0:T(1,128)S(1)}, u32[]{:S(2)}, u32[]{:S(2)}) collective-permute-start(s32[8,1,128]{2,1,0:T(1,128)S(1)} %get-tuple-element.55), channel_id=1, source_target_pairs={{8,0},{16,8},{24,16},{0,24},{9,1},{17,9},{25,17},{1,25},{10,2},{18... | collective-permute-start | bytes 12296 | tf_op jit(solution)/shard_map/ppermute | solution.py:20
  9.1 8.7 %copy-start.1 = (s32[8,64,128]{2,1,0:T(8,128)S(1)}, s32[8,64,128]{2,1,0:T(8,128)}, u32[]{:S(2)}) copy-start(s32[8,64,128]{2,1,0:T(8,128)} %param.3) | copy-start | bytes 786436
  9.3 7.4 %collective-permute-start.2 = (s32[8,66,1]{2,1,0:T(8,128)S(1)}, s32[8,66,1]{2,1,0:T(8,128)S(1)}, u32[]{:S(2)}, u32[]{:S(2)}) collective-permute-start(s32[8,66,1]{2,1,0:T(8,128)S(1)} %get-tuple-element.46), channel_id=1, source_target_pairs={{0,2},{2,4},{4,6},{6,0},{1,3},{3,5},{5,7},{7,1},{8,10},{10,12},{12... | collective-permute-start | bytes 6344 | tf_op jit(solution)/shard_map/ppermute | solution.py:18
  9.3 8.5 %collective-permute-start.3 = (s32[8,66,1]{2,1,0:T(8,128)S(1)}, s32[8,66,1]{2,1,0:T(8,128)S(1)}, u32[]{:S(2)}, u32[]{:S(2)}) collective-permute-start(s32[8,66,1]{2,1,0:T(8,128)S(1)} %get-tuple-element.47), channel_id=1, source_target_pairs={{2,0},{4,2},{6,4},{0,6},{3,1},{5,3},{7,5},{1,7},{10,8},{12,10},{14... | collective-permute-start | bytes 6344 | tf_op jit(solution)/shard_map/ppermute | solution.py:20
  18.0 5.0 %collective-permute-start.4 = (s32[1,66,130]{2,1,0:T(8,128)S(1)}, s32[1,66,130]{2,1,0:T(8,128)S(1)}, u32[]{:S(2)}, u32[]{:S(2)}) collective-permute-start(s32[1,66,130]{2,1,0:T(8,128)S(1)} %get-tuple-element.38), channel_id=1, source_target_pairs={{0,1},{1,0},{2,3},{3,2},{4,5},{5,4},{6,7},{7,6},{8,9},{9,8},{10,11... | collective-permute-start | bytes 102968 | tf_op jit(solution)/shard_map/ppermute | solution.py:18
  19.5 5.2 %copy-start = (bf16[8,64,128]{2,1,0:T(8,128)(2,1)S(1)}, bf16[8,64,128]{2,1,0:T(8,128)(2,1)}, u32[]{:S(2)}) copy-start(bf16[8,64,128]{2,1,0:T(8,128)(2,1)} %param.2) | copy-start | bytes 393220
  19.5 4.9 %collective-permute-start.5 = (s32[1,66,130]{2,1,0:T(8,128)S(1)}, s32[1,66,130]{2,1,0:T(8,128)S(1)}, u32[]{:S(2)}, u32[]{:S(2)}) collective-permute-start(s32[1,66,130]{2,1,0:T(8,128)S(1)} %get-tuple-element.39), channel_id=1, source_target_pairs={{1,0},{0,1},{3,2},{2,3},{5,4},{4,5},{7,6},{6,7},{9,8},{8,9},{11,10... | collective-permute-start | bytes 102968 | tf_op jit(solution)/shard_map/ppermute | solution.py:20
  25.3 5.5 %collective-permute-start.6 = (bf16[8,1,128]{2,1,0:T(2,128)(2,1)S(1)}, bf16[8,1,128]{2,1,0:T(2,128)(2,1)S(1)}, u32[]{:S(2)}, u32[]{:S(2)}) collective-permute-start(bf16[8,1,128]{2,1,0:T(2,128)(2,1)S(1)} %get-tuple-element.58), channel_id=1, source_target_pairs={{0,8},{8,16},{16,24},{24,0},{1,9},{9,17},{17,25},{25,1},{2,10},{10... | collective-permute-start | bytes 6152 | tf_op jit(solution)/shard_map/ppermute | solution.py:18
  26.9 3.9 %collective-permute-start.7 = (bf16[8,1,128]{2,1,0:T(2,128)(2,1)S(1)}, bf16[8,1,128]{2,1,0:T(2,128)(2,1)S(1)}, u32[]{:S(2)}, u32[]{:S(2)}) collective-permute-start(bf16[8,1,128]{2,1,0:T(2,128)(2,1)S(1)} %get-tuple-element.59), channel_id=1, source_target_pairs={{8,0},{16,8},{24,16},{0,24},{9,1},{17,9},{25,17},{1,25},{10,2},{18... | collective-permute-start | bytes 6152 | tf_op jit(solution)/shard_map/ppermute | solution.py:20
  30.9 4.6 %collective-permute-start.8 = (bf16[8,66,1]{2,1,0:T(8,128)(2,1)S(1)}, bf16[8,66,1]{2,1,0:T(8,128)(2,1)S(1)}, u32[]{:S(2)}, u32[]{:S(2)}) collective-permute-start(bf16[8,66,1]{2,1,0:T(8,128)(2,1)S(1)} %get-tuple-element.56), channel_id=1, source_target_pairs={{0,2},{2,4},{4,6},{6,0},{1,3},{3,5},{5,7},{7,1},{8,10},{10,12},{12... | collective-permute-start | bytes 3176 | tf_op jit(solution)/shard_map/ppermute | solution.py:18
  31.0 5.3 %collective-permute-start.9 = (bf16[8,66,1]{2,1,0:T(8,128)(2,1)S(1)}, bf16[8,66,1]{2,1,0:T(8,128)(2,1)S(1)}, u32[]{:S(2)}, u32[]{:S(2)}) collective-permute-start(bf16[8,66,1]{2,1,0:T(8,128)(2,1)S(1)} %get-tuple-element.57), channel_id=1, source_target_pairs={{2,0},{4,2},{6,4},{0,6},{3,1},{5,3},{7,5},{1,7},{10,8},{12,10},{14... | collective-permute-start | bytes 3176 | tf_op jit(solution)/shard_map/ppermute | solution.py:20
  36.4 4.4 %collective-permute-start.10 = (bf16[1,66,130]{2,1,0:T(8,128)(2,1)S(1)}, bf16[1,66,130]{2,1,0:T(8,128)(2,1)S(1)}, u32[]{:S(2)}, u32[]{:S(2)}) collective-permute-start(bf16[1,66,130]{2,1,0:T(8,128)(2,1)S(1)} %get-tuple-element.40), channel_id=1, source_target_pairs={{0,1},{1,0},{2,3},{3,2},{4,5},{5,4},{6,7},{7,6},{8,9},{9,8},{10,11... | collective-permute-start | bytes 51488 | tf_op jit(solution)/shard_map/ppermute | solution.py:18
  38.0 4.1 %collective-permute-start.11 = (bf16[1,66,130]{2,1,0:T(8,128)(2,1)S(1)}, bf16[1,66,130]{2,1,0:T(8,128)(2,1)S(1)}, u32[]{:S(2)}, u32[]{:S(2)}) collective-permute-start(bf16[1,66,130]{2,1,0:T(8,128)(2,1)S(1)} %get-tuple-element.41), channel_id=1, source_target_pairs={{1,0},{0,1},{3,2},{2,3},{5,4},{4,5},{7,6},{6,7},{9,8},{8,9},{11,10... | collective-permute-start | bytes 51488 | tf_op jit(solution)/shard_map/ppermute | solution.py:20
  43.5 5.5 %collective-permute-start.12 = (f32[8,1,128]{2,1,0:T(1,128)S(1)}, f32[8,1,128]{2,1,0:T(1,128)S(1)}, u32[]{:S(2)}, u32[]{:S(2)}) collective-permute-start(f32[8,1,128]{2,1,0:T(1,128)S(1)} %get-tuple-element.52), channel_id=1, source_target_pairs={{0,8},{8,16},{16,24},{24,0},{1,9},{9,17},{17,25},{25,1},{2,10},{10... | collective-permute-start | bytes 12296 | tf_op jit(solution)/shard_map/ppermute | solution.py:18
  44.7 4.3 %collective-permute-start.13 = (f32[8,1,128]{2,1,0:T(1,128)S(1)}, f32[8,1,128]{2,1,0:T(1,128)S(1)}, u32[]{:S(2)}, u32[]{:S(2)}) collective-permute-start(f32[8,1,128]{2,1,0:T(1,128)S(1)} %get-tuple-element.53), channel_id=1, source_target_pairs={{8,0},{16,8},{24,16},{0,24},{9,1},{17,9},{25,17},{1,25},{10,2},{18... | collective-permute-start | bytes 12296 | tf_op jit(solution)/shard_map/ppermute | solution.py:20
  49.2 7.5 %collective-permute-start.14 = (f32[8,66,1]{2,1,0:T(8,128)S(1)}, f32[8,66,1]{2,1,0:T(8,128)S(1)}, u32[]{:S(2)}, u32[]{:S(2)}) collective-permute-start(f32[8,66,1]{2,1,0:T(8,128)S(1)} %get-tuple-element.44), channel_id=1, source_target_pairs={{0,2},{2,4},{4,6},{6,0},{1,3},{3,5},{5,7},{7,1},{8,10},{10,12},{12... | collective-permute-start | bytes 6344 | tf_op jit(solution)/shard_map/ppermute | solution.py:18
  49.3 8.3 %collective-permute-start.15 = (f32[8,66,1]{2,1,0:T(8,128)S(1)}, f32[8,66,1]{2,1,0:T(8,128)S(1)}, u32[]{:S(2)}, u32[]{:S(2)}) collective-permute-start(f32[8,66,1]{2,1,0:T(8,128)S(1)} %get-tuple-element.45), channel_id=1, source_target_pairs={{2,0},{4,2},{6,4},{0,6},{3,1},{5,3},{7,5},{1,7},{10,8},{12,10},{14... | collective-permute-start | bytes 6344 | tf_op jit(solution)/shard_map/ppermute | solution.py:20
  57.6 0.7 copy-start.4
  58.3 30.3 %collective-permute-start.16 = (f32[1,66,130]{2,1,0:T(8,128)S(1)}, f32[1,66,130]{2,1,0:T(8,128)S(1)}, u32[]{:S(2)}, u32[]{:S(2)}) collective-permute-start(f32[1,66,130]{2,1,0:T(8,128)S(1)} %get-tuple-element.36), channel_id=1, source_target_pairs={{0,1},{1,0},{2,3},{3,2},{4,5},{5,4},{6,7},{7,6},{8,9},{9,8},{10,11... | collective-permute-start | bytes 102968 | tf_op jit(solution)/shard_map/ppermute | solution.py:18
  59.2 29.5 %collective-permute-start.17 = (f32[1,66,130]{2,1,0:T(8,128)S(1)}, f32[1,66,130]{2,1,0:T(8,128)S(1)}, u32[]{:S(2)}, u32[]{:S(2)}) collective-permute-start(f32[1,66,130]{2,1,0:T(8,128)S(1)} %get-tuple-element.37), channel_id=1, source_target_pairs={{1,0},{0,1},{3,2},{2,3},{5,4},{4,5},{7,6},{6,7},{9,8},{8,9},{11,10... | collective-permute-start | bytes 102968 | tf_op jit(solution)/shard_map/ppermute | solution.py:20
  90.1 5.5 %collective-permute-start.18 = (f32[8,1,128]{2,1,0:T(1,128)S(1)}, f32[8,1,128]{2,1,0:T(1,128)S(1)}, u32[]{:S(2)}, u32[]{:S(2)}) collective-permute-start(f32[8,1,128]{2,1,0:T(1,128)S(1)} %get-tuple-element.50), channel_id=1, source_target_pairs={{0,8},{8,16},{16,24},{24,0},{1,9},{9,17},{17,25},{25,1},{2,10},{10... | collective-permute-start | bytes 12296 | tf_op jit(solution)/shard_map/ppermute | solution.py:18
  90.2 5.4 %collective-permute-start.19 = (f32[8,1,128]{2,1,0:T(1,128)S(1)}, f32[8,1,128]{2,1,0:T(1,128)S(1)}, u32[]{:S(2)}, u32[]{:S(2)}) collective-permute-start(f32[8,1,128]{2,1,0:T(1,128)S(1)} %get-tuple-element.51), channel_id=1, source_target_pairs={{8,0},{16,8},{24,16},{0,24},{9,1},{17,9},{25,17},{1,25},{10,2},{18... | collective-permute-start | bytes 12296 | tf_op jit(solution)/shard_map/ppermute | solution.py:20
  95.8 8.3 %collective-permute-start.20 = (f32[8,66,1]{2,1,0:T(8,128)S(1)}, f32[8,66,1]{2,1,0:T(8,128)S(1)}, u32[]{:S(2)}, u32[]{:S(2)}) collective-permute-start(f32[8,66,1]{2,1,0:T(8,128)S(1)} %get-tuple-element.42), channel_id=1, source_target_pairs={{0,2},{2,4},{4,6},{6,0},{1,3},{3,5},{5,7},{7,1},{8,10},{10,12},{12... | collective-permute-start | bytes 6344 | tf_op jit(solution)/shard_map/ppermute | solution.py:18
  95.9 8.2 %collective-permute-start.21 = (f32[8,66,1]{2,1,0:T(8,128)S(1)}, f32[8,66,1]{2,1,0:T(8,128)S(1)}, u32[]{:S(2)}, u32[]{:S(2)}) collective-permute-start(f32[8,66,1]{2,1,0:T(8,128)S(1)} %get-tuple-element.43), channel_id=1, source_target_pairs={{2,0},{4,2},{6,4},{0,6},{3,1},{5,3},{7,5},{1,7},{10,8},{12,10},{14... | collective-permute-start | bytes 6344 | tf_op jit(solution)/shard_map/ppermute | solution.py:20
  104.1 0.7 copy-start.2
  104.1 0.8 copy-start.3
  104.9 34.5 %collective-permute-start.22 = (f32[1,66,130]{2,1,0:T(8,128)S(1)}, f32[1,66,130]{2,1,0:T(8,128)S(1)}, u32[]{:S(2)}, u32[]{:S(2)}) collective-permute-start(f32[1,66,130]{2,1,0:T(8,128)S(1)} %get-tuple-element.34), channel_id=1, source_target_pairs={{0,1},{1,0},{2,3},{3,2},{4,5},{5,4},{6,7},{7,6},{8,9},{9,8},{10,11... | collective-permute-start | bytes 102968 | tf_op jit(solution)/shard_map/ppermute | solution.py:18
  105.7 33.8 %collective-permute-start.23 = (f32[1,66,130]{2,1,0:T(8,128)S(1)}, f32[1,66,130]{2,1,0:T(8,128)}, u32[]{:S(2)}, u32[]{:S(2)}) collective-permute-start(f32[1,66,130]{2,1,0:T(8,128)S(1)} %get-tuple-element.35), channel_id=1, source_target_pairs={{1,0},{0,1},{3,2},{2,3},{5,4},{4,5},{7,6},{6,7},{9,8},{8,9},{11,10... | collective-permute-start | bytes 102968 | tf_op jit(solution)/shard_map/ppermute | solution.py:20
  139.5 0.6 copy-start.5
